TPU v7x, 32 devices: a whole 2x2x4 slice. The times are simulated.
32 devices in a mesh: cell: 16 (over z, y, x), pre: 2 (over core).
Axes of the slice: x: 2, y: 2, z: 4, core: 2. Of those that a mesh axis runs over, the one named last changes fastest.
Arguments:
- v_init: float32 [128, 16, 4096], P(None, None, ('cell', 'pre')), may hold values from -6 to 6
- cotangent: float32 [128, 16, 4096], P(None, None, ('cell', 'pre')), may hold values from -6 to 6
- weights: bfloat16 [4096, 4096], P('cell', 'pre'), may hold values from -2 to 2
- leak: float32 [4096], P(('cell', 'pre')), may hold values from 0.2 to 1.5
- drive: float32 [4096], P(('cell', 'pre')), may hold values from 0.5 to 2
- site: int32 [4096], P(('cell', 'pre')), may hold values from 0 to 127
- parent: int32 [128], replicated, may hold values from 0 to 126, as said below
- axial: float32 [128], replicated, may hold values from 1 to 8
- cap: float32 [128], replicated, may hold values from 2 to 6
- bank: float32 [16, 128], replicated, may hold values from -5 to 5
- sched: int32 [2, 16], replicated, may hold values from 0 to 15
Outputs:
- v_final: float32 [128, 16, 4096], P(None, None, ('cell', 'pre'))
- v_grad: float32 [128, 16, 4096], P(None, None, ('cell', 'pre'))
Inputs may be any that keep to these rules, and one draw needn't show every extreme that they name: parent[0] = 0, and for i >= 1 parent[i] < i and i - parent[i] <= 8.
All inputs are finite; a program needn't handle non-finite values.
Results may differ from a plain program's by a relative error of at most 0.0021.
Values may be sent and summed in bfloat16 or wider, within the bound.
A program may use at most 64 MiB of HBM per device.

v0:
```python
import jax
import jax.numpy as jnp
from jax import lax
from jax.sharding import PartitionSpec as P

reversal = 1.0


def tree_inverse(parent, axial, cap):
    length = parent.shape[0]
    indices = jnp.arange(length, dtype=jnp.int32)
    onehot = (parent[:, None] == indices[None, :]).astype(jnp.float32)
    ident = jnp.eye(length, dtype=jnp.float32)
    edges = (ident - onehot) * (indices > 0).astype(jnp.float32)[:, None]
    shunt = axial * (indices == 0).astype(jnp.float32)
    system = jnp.diag(cap + shunt) + jnp.dot(
        edges.T * axial[None, :], edges, precision=lax.Precision.HIGHEST
    )
    lower = jnp.linalg.cholesky(system)
    factor = lax.linalg.triangular_solve(lower, ident, left_side=True, lower=True)
    return jnp.dot(factor.T, factor, precision=lax.Precision.HIGHEST)


def apply_matrix(matrix, field):
    depth, trials, cells = field.shape
    flat = jnp.dot(matrix, field.reshape(depth, trials * cells), precision=lax.Precision.HIGHEST)
    return flat.reshape(depth, trials, cells)


def forward_drive(activity, weights):
    partial_rows = lax.dot_general(
        lax.all_gather(activity, "cell", axis=1, tiled=True),
        weights,
        (((1,), (1,)), ((), ())),
        preferred_element_type=jnp.float32,
    )
    return lax.psum_scatter(partial_rows, "pre", scatter_dimension=1, tiled=True)


def backward_drive(site_adjoint, weights):
    partial_cols = jnp.dot(
        lax.all_gather(site_adjoint, "pre", axis=1, tiled=True),
        weights,
        preferred_element_type=jnp.float32,
    )
    return lax.psum_scatter(partial_cols, "cell", scatter_dimension=1, tiled=True)


def body(v_init, cotangent, weights, leak, drive, site, parent, axial, cap, bank, sched):
    inverse = tree_inverse(parent, axial, cap)
    depth = parent.shape[0]
    comps = jnp.arange(depth, dtype=jnp.int32)
    mask = (site[None, :] == comps[:, None]).astype(jnp.float32)
    levels = cap[:, None, None] - leak[None, None, :]
    select = (
        sched[:, :, None] == jnp.arange(bank.shape[0], dtype=jnp.int32)[None, None, :]
    ).astype(jnp.float32)
    field = v_init
    saved = []
    for moment in range(sched.shape[0]):
        rates = jax.nn.sigmoid(field[0])
        activity = rates.astype(jnp.bfloat16)
        synaptic = forward_drive(activity, weights)
        pattern = jnp.dot(select[moment], bank, precision=lax.Precision.HIGHEST)
        source = pattern.T[:, :, None] * drive[None, None, :]
        total = levels * field + mask[:, None, :] * synaptic[None] * (reversal - field) + source
        saved.append((field, rates, synaptic))
        field = apply_matrix(inverse, total)
    adjoint = cotangent
    for moment in range(sched.shape[0] - 1, -1, -1):
        state, rates, synaptic = saved[moment]
        pulled = apply_matrix(inverse.T, adjoint)
        site_adjoint = jnp.sum(mask[:, None, :] * pulled * (reversal - state), axis=0).astype(
            jnp.bfloat16
        )
        returned = backward_drive(site_adjoint, weights)
        adjoint = levels * pulled - mask[:, None, :] * synaptic[None] * pulled
        adjoint = adjoint.at[0].add(returned * rates * (1.0 - rates))
    return (field, adjoint)


def solution(mesh):
    in_specs = (
        P(None, None, ("cell", "pre")),
        P(None, None, ("cell", "pre")),
        P("cell", "pre"),
        P(("cell", "pre")),
        P(("cell", "pre")),
        P(("cell", "pre")),
        P(),
        P(),
        P(),
        P(),
        P(),
    )
    out_specs = (P(None, None, ("cell", "pre")), P(None, None, ("cell", "pre")))
    return jax.shard_map(body, mesh=mesh, in_specs=in_specs, out_specs=out_specs, check_vma=False)
```

profile of v0, /device:TPU:0, one launch (start us, length us, event | category | flops | bytes accessed | tf_op | source)
XLA Modules:
  0.0 310.3 jit_solution(1017453609851802560)
XLA Ops:
  7.2 0.8 bitcast_convert_fusion
  8.0 42.7 %all_gather.12 = bf16[16,2048]{1,0:T(8,128)(2,1)S(1)} all-gather(bf16[16,128]{1,0:T(8,128)(2,1)S(1)} %bitcast_convert_fusion), channel_id=1, replica_groups=mesh['cell'=16,'pre'=2] {'cell'}, dimensions={1}, use_global_device_ids=true | all-gather | bytes 69632 | tf_op jit(solution)/shard_map/all_gather | solution.py:32
  50.8 1.0 fusion.42
  51.8 0.6 copy-done.7
  52.5 0.6 copy-done.8
  53.1 0.6 copy-done.9
  53.8 0.6 copy-done.10
  54.5 0.6 copy-done.11
  55.1 0.3 fusion.19
  55.6 11.7 %cholesky.18 = f32[128,128]{1,0:T(8,128)S(1)} custom-call(f32[128,128]{1,0:T(8,128)S(1)} %fusion.18), custom_call_target="Cholesky" | custom-call | tf_op jit(solution)/shard_map/jit(cholesky)/cholesky | solution.py:19
  67.3 0.6 compare_reduce_fusion
  68.0 0.7 fusion.8
  68.6 9.8 %custom-call.6 = f32[1,128,128]{1,2,0:T(8,128)S(1)} custom-call(f32[1,128,128]{2,1,0:T(8,128)S(1)} %fusion.8), custom_call_target="InvertDiagBlocksLowerTriangular" | custom-call | tf_op jit(solution)/shard_map/triangular_solve | solution.py:20
  78.5 0.2 fusion.15
  78.7 0.3 fusion.41
  79.0 0.4 copy-done.5
  79.4 0.1 convolution_bitcast_fusion
  79.5 0.1 convolution_bitcast_fusion.1
  79.7 0.5 copy-done.6
  80.2 1.1 fusion.1
  81.3 1.3 copy.35
  82.6 2.2 fusion.43
  84.9 35.8 %all_gather.13 = bf16[16,2048]{1,0:T(8,128)(2,1)S(1)} all-gather(bf16[16,128]{1,0:T(8,128)(2,1)S(1)} %convert_element_type.49), channel_id=1, replica_groups=mesh['cell'=16,'pre'=2] {'cell'}, dimensions={1}, use_global_device_ids=true | all-gather | bytes 69632 | tf_op jit(solution)/shard_map/all_gather | solution.py:32
  120.7 1.0 fusion.44
  121.7 0.2 reduce-scatter.9.cloned.1.call-start
  122.0 0.1 copy.37
  122.1 2.5 copy.77
  124.6 2.6 copy.39
  127.2 0.3 mul.199
  127.7 0.6 copy-done.4
  128.3 2.9 subtract_bitcast_fusion
  131.2 2.6 copy.52
  133.8 3.3 %fusion.7 = (bf16[16,128]{1,0:T(8,128)(2,1)S(1)}, f32[128,16,128]{2,0,1:T(8,128)}) fusion(f32[16,16,8,128]{3,2,1,0:T(8,128)} %get-tuple-element.32, f32[128,128]{1,0:T(8,128)S(1)} %fusion.29, f32[16,128,128]{2,1,0:T(8,128)S(1)} %bitcast.115, f32[128,128]{1,0:T(8,128)S(1)} %fusion.41), kind=kOutput, calls=%fused_computation.17 | convolution fusion | flops 403437568 | bytes 3280896 | tf_op jit(solution)/shard_map/dot_general | solution.py:26
  137.1 1.8 all_gather.14
  139.0 0.9 fusion.45
  140.0 1.9 multiply_subtract_fusion
  141.9 76.3 %reduce-scatter.9.cloned.1.call-done = f32[16,128]{1,0:T(8,128)} async-done(((f32[16,2048]{1,0:T(8,128)}), f32[16,128]{1,0:T(8,128)}) %reduce-scatter.9.cloned.1.call-update) | async-done | bytes 8208 | tf_op jit(solution)/shard_map/reduce_scatter | solution.py:46
  218.2 0.7 fusion.35
  218.9 1.3 copy.76
  220.2 2.5 copy.46
  222.7 2.6 multiply_reduce_fusion
  225.4 1.8 all_gather.15
  227.2 0.9 fusion.46
  228.2 2.2 fusion.13
  230.4 1.6 copy.48
  232.0 69.4 %reduce-scatter.11.cloned.1.call-done = f32[16,128]{1,0:T(8,128)} async-done(((f32[16,2048]{1,0:T(8,128)}), f32[16,128]{1,0:T(8,128)}) %reduce-scatter.11.cloned.1.call-update) | async-done | bytes 8208 | tf_op jit(solution)/shard_map/reduce_scatter | solution.py:46
  301.4 0.7 fusion.39
  302.2 1.6 copy.49
  (42 shorter events, 0.9 us)
Async XLA Ops:
  7.2 43.6 %copy-start = (bf16[256,2048]{1,0:T(8,128)(2,1)S(1)}, bf16[256,2048]{1,0:T(8,128)(2,1)}, u32[]{:S(2)}) copy-start(bf16[256,2048]{1,0:T(8,128)(2,1)} %param.17) | copy-start | bytes 3145732
  7.2 72.5 %reduce-scatter.5.cloned.1.call-start = ((), (), s32[]{:S(2)}) async-start(), calls=%async_computation.4 | async-start | bytes 24576 | tf_op jit(solution)/shard_map/reduce_scatter | solution.py:37
  50.8 28.9 %copy-start.1 = (f32[128,16,128]{2,1,0:T(8,128)S(1)}, f32[128,16,128]{2,1,0:T(8,128)}, u32[]{:S(2)}) copy-start(f32[128,16,128]{2,1,0:T(8,128)} %param.15) | copy-start | bytes 3145732
  51.8 0.7 copy-start.7
  51.8 75.4 %reduce-scatter.7.cloned.1.call-start = ((), (), s32[]{:S(2)}) async-start(), calls=%async_computation.5 | async-start | bytes 24576 | tf_op jit(solution)/shard_map/reduce_scatter | solution.py:37
  52.5 0.7 copy-start.8
  53.1 0.7 copy-start.9
  53.1 0.7 copy-start.12
  53.8 0.7 copy-start.10
  54.4 0.7 copy-start.11
  78.7 0.7 copy-start.5
  79.5 0.7 copy-start.6
  121.7 96.4 %reduce-scatter.9.cloned.1.call-start = ((), (), s32[]{:S(2)}) async-start(), calls=%async_computation.6 | async-start | bytes 139264 | tf_op jit(solution)/shard_map/reduce_scatter | solution.py:46
  127.6 0.7 copy-start.4
  131.2 2.6 copy-start.2
  139.9 161.5 %reduce-scatter.11.cloned.1.call-start = ((), (), s32[]{:S(2)}) async-start(), calls=%async_computation.7 | async-start | bytes 139264 | tf_op jit(solution)/shard_map/reduce_scatter | solution.py:46
  220.2 2.5 copy-start.3
Sparse Core Ops, SparseCore 0:
  51.9 3.4 reduce-scatter.4
  121.9 5.2 reduce-scatter.6
  140.0 78.0 reduce-scatter.8
  228.3 73.1 reduce-scatter.10
where the time goes:
time: 311 us; the launch traced here: 310 us
  waiting for transfers between devices  146 us (47%)
  blocking collectives  82.2 us (26%)
  other arithmetic  31.3 us (10%)
  local copies, waits for them, and re-layouts  21.4 us (7%)
  matrix products  15.3 us (5%)
  between operations  14 us (5%)
    reduce_scatter x2, waiting for transfers between devices, backward_drive(): lax.psum_scatter(partial_cols, 'cell', scatter_dimension=1, tiled=True)  146 us
    all_gather x2, blocking collectives, forward_drive(): lax.all_gather(activity, 'cell', axis=1, tiled=True)  78.5 us
    another operation x3, other arithmetic, tree_inverse(): lower = jnp.linalg.cholesky(system)  12.4 us
    unnamed x30, local copies, waits for them, and re-layouts  11.7 us
    another operation x2, other arithmetic, tree_inverse(): lax.linalg.triangular_solve(lower, ident, left_side=True, lower=True)  10.5 us
    dot_general x4, matrix products, apply_matrix(): jnp.dot(matrix, field.reshape(depth, trials * cells), precision=lax.Preci...  10.4 us
    dot_general x3, local copies, waits for them, and re-layouts, apply_matrix(): jnp.dot(matrix, field.reshape(depth, trials * cells), precision=lax.Preci...  7.73 us
  transfers between devices with their start and end apart: 4, of which 2 were waited for; matrix products, arithmetic and copies ran while one was open for 11% of the time, Pallas kernels for 0%

commit v1 on v0

--- a/solution.py
+++ b/solution.py
@@ -28,8 +28,11 @@
 
 
 def forward_drive(activity, weights):
+    plan_point = lambda frame, array_dim: jnp.concatenate(
+        lax.all_to_all(jnp.stack([frame] * lax.axis_size("cell")), "cell", 0, 0), axis=array_dim
+    )
     partial_rows = lax.dot_general(
-        lax.all_gather(activity, "cell", axis=1, tiled=True),
+        plan_point(activity, 1),
         weights,
         (((1,), (1,)), ((), ())),
         preferred_element_type=jnp.float32,

time: 311 us -> 263 us (0.85)
  blocking collectives: 82.2 us -> 3.67 us
  starting transfers between devices: 0.34 us -> 15.4 us
  waiting for transfers between devices: 146 us -> 160 us
    all_gather x2 -> x0, blocking collectives: 78.5 us -> none  [forward_drive(): lax.all_gather(activity, 'cell', axis=1, tiled=True)]
    all_to_all x0 -> x2, starting transfers between devices: none -> 15.1 us  [forward_drive(): lax.all_to_all(jnp.stack([frame] * lax.axis_size('cell')), 'cell', 0, 0)]
    reduce_scatter x2, waiting for transfers between devices: 0.01 us -> 8.16 us  [forward_drive(): lax.psum_scatter(partial_rows, 'pre', scatter_dimension=1, tiled=True)]
    all_to_all x0 -> x2, waiting for transfers between devices: none -> 7.37 us  [forward_drive(): lax.all_to_all(jnp.stack([frame] * lax.axis_size('cell')), 'cell', 0, 0)]
  transfers between devices with their start and end apart: 4 -> 6, of which waited for: 2 -> 4; matrix products, arithmetic and copies ran while one was open for 11% -> 13% of each run, Pallas kernels for 0% -> 0%
where the time goes in v1:
time: 263 us; the launch traced here: 262 us
  waiting for transfers between devices  160 us (61%)
  other arithmetic  31.3 us (12%)
  local copies, waits for them, and re-layouts  21.8 us (8%)
  starting transfers between devices  15.4 us (6%)
  matrix products  15.3 us (6%)
  between operations  14 us (5%)
  blocking collectives  3.67 us (1%)
    reduce_scatter x2, waiting for transfers between devices, backward_drive(): lax.psum_scatter(partial_cols, 'cell', scatter_dimension=1, tiled=True)  145 us
    all_to_all x2, starting transfers between devices, forward_drive(): lax.all_to_all(jnp.stack([frame] * lax.axis_size('cell')), 'cell', 0, 0)  15.1 us
    another operation x3, other arithmetic, tree_inverse(): lower = jnp.linalg.cholesky(system)  12.4 us
    unnamed x30, local copies, waits for them, and re-layouts  10.8 us
    another operation x2, other arithmetic, tree_inverse(): lax.linalg.triangular_solve(lower, ident, left_side=True, lower=True)  10.5 us
    dot_general x4, matrix products, apply_matrix(): jnp.dot(matrix, field.reshape(depth, trials * cells), precision=lax.Preci...  10.4 us
    reduce_scatter x2, waiting for transfers between devices, forward_drive(): lax.psum_scatter(partial_rows, 'pre', scatter_dimension=1, tiled=True)  8.16 us
    dot_general x3, local copies, waits for them, and re-layouts, apply_matrix(): jnp.dot(matrix, field.reshape(depth, trials * cells), precision=lax.Preci...  7.75 us
  transfers between devices with their start and end apart: 6, of which 4 were waited for; matrix products, arithmetic and copies ran while one was open for 13% of the time, Pallas kernels for 0%

profile of v1, /device:TPU:0, one launch (start us, length us, event | category | flops | bytes accessed | tf_op | source)
XLA Modules:
  0.0 261.7 jit_solution(16319705810611774636)
XLA Ops:
  7.2 0.8 convert_bitcast_fusion
  8.0 0.6 stack.7
  8.6 8.3 %all-to-all-start = ((bf16[16,16,128]{2,1,0:T(8,128)(2,1)}), bf16[16,16,128]{2,1,0:T(8,128)(2,1)S(1)}, u32[]{:S(2)}, u32[]{:S(2)}) async-start(bf16[16,16,128]{2,1,0:T(8,128)(2,1)} %stack.7), calls=%async_computation | async-start | bytes 131072 | tf_op jit(solution)/shard_map/all_to_all | solution.py:32
  17.0 0.6 copy-done.8
  17.6 0.6 copy-done.9
  18.3 0.6 copy-done.10
  19.0 0.6 copy-done.11
  19.6 0.3 fusion.25
  20.1 11.7 %cholesky.18 = f32[128,128]{1,0:T(8,128)S(1)} custom-call(f32[128,128]{1,0:T(8,128)S(1)} %fusion.24), custom_call_target="Cholesky" | custom-call | tf_op jit(solution)/shard_map/jit(cholesky)/cholesky | solution.py:19
  31.9 0.6 compare_reduce_fusion
  32.5 0.7 fusion.8
  33.2 9.8 %custom-call.6 = f32[1,128,128]{1,2,0:T(8,128)S(1)} custom-call(f32[1,128,128]{2,1,0:T(8,128)S(1)} %fusion.8), custom_call_target="InvertDiagBlocksLowerTriangular" | custom-call | tf_op jit(solution)/shard_map/triangular_solve | solution.py:20
  43.0 0.2 fusion.21
  43.2 0.3 fusion.47
  43.6 1.0 fusion.12
  44.6 0.7 copy-done.5
  45.4 8.2 %reduce-scatter.5.cloned.1.call-done = f32[16,128]{1,0:T(8,128)} async-done(((f32[16,256]{1,0:T(8,128)}), f32[16,128]{1,0:T(8,128)}) %reduce-scatter.5.cloned.1.call-update) | async-done | bytes 8208 | tf_op jit(solution)/shard_map/reduce_scatter | solution.py:40
  53.6 1.1 fusion.1
  54.7 1.3 copy.55
  56.0 2.2 fusion.48
  58.3 0.6 stack.8
  59.0 6.7 %all-to-all-start.1 = ((bf16[16,16,128]{2,1,0:T(8,128)(2,1)}), bf16[16,16,128]{2,1,0:T(8,128)(2,1)S(1)}, u32[]{:S(2)}, u32[]{:S(2)}) async-start(bf16[16,16,128]{2,1,0:T(8,128)(2,1)} %stack.8), calls=%async_computation.2 | async-start | bytes 131072 | tf_op jit(solution)/shard_map/all_to_all | solution.py:32
  65.8 0.1 convolution_bitcast_fusion
  65.9 7.4 %all-to-all-done.1 = bf16[16,16,128]{2,1,0:T(8,128)(2,1)S(1)} async-done(((bf16[16,16,128]{2,1,0:T(8,128)(2,1)}), bf16[16,16,128]{2,1,0:T(8,128)(2,1)S(1)}, u32[]{:S(2)}, u32[]{:S(2)}) %all-to-all-start.1) | async-done | bytes 65568 | tf_op jit(solution)/shard_map/all_to_all | solution.py:32
  73.3 1.0 fusion.9
  74.3 0.2 reduce-scatter.9.cloned.1.call-start
  74.6 2.5 copy.108
  77.1 2.6 copy.60
  79.7 0.3 mul.199
  80.2 0.6 copy-done.4
  80.8 2.9 %subtract_bitcast_fusion = (f32[16,16,8,128]{3,2,1,0:T(8,128)}, f32[2048,128]{0,1:T(8,128)}) fusion(f32[128,2048]{1,0:T(8,128)S(1)} %fusion.48, f32[2048]{0:T(1024)S(1)} %broadcast_bitcast_fusion, f32[16,8,16,128]{3,2,1,0:T(8,128)S(1)} %bitcast.135, f32[2048]{0:T(1024)S(1)} %bitcast.141, f32[16,8,16,128]{3,2,1,0:T(8,128)S(1)} %bitcast.137, ...), kind=kLoop, calls=%fused_computation.21 | loop fusion | flops 1835008 | bytes 6307840
  83.8 2.6 copy.73
  86.4 3.3 %fusion.7 = (bf16[16,128]{1,0:T(8,128)(2,1)S(1)}, f32[128,16,128]{2,0,1:T(8,128)}) fusion(f32[16,16,8,128]{3,2,1,0:T(8,128)} %get-tuple-element.34, f32[128,128]{1,0:T(8,128)S(1)} %fusion.35, f32[16,128,128]{2,1,0:T(8,128)S(1)} %bitcast.130, f32[128,128]{1,0:T(8,128)S(1)} %fusion.47), kind=kOutput, calls=%fused_computation.17 | convolution fusion | flops 403437568 | bytes 3280896 | tf_op jit(solution)/shard_map/dot_general | solution.py:26
  89.7 1.8 all_gather.6
  91.5 0.9 fusion.49
  92.5 1.9 multiply_subtract_fusion
  94.4 75.1 %reduce-scatter.9.cloned.1.call-done = f32[16,128]{1,0:T(8,128)} async-done(((f32[16,2048]{1,0:T(8,128)}), f32[16,128]{1,0:T(8,128)}) %reduce-scatter.9.cloned.1.call-update) | async-done | bytes 8208 | tf_op jit(solution)/shard_map/reduce_scatter | solution.py:49
  169.5 0.7 fusion.41
  170.2 1.3 copy.107
  171.5 2.5 copy.67
  174.0 2.6 %multiply_reduce_fusion = (bf16[16,128]{1,0:T(8,128)(2,1)S(1)}, f32[128,16,128]{2,0,1:T(8,128)S(1)}) fusion(f32[128,16,128]{2,1,0:T(8,128)S(1)} %copy-done.1, f32[128,128]{1,0:T(8,128)S(1)} %fusion.35, f32[16,128]{1,0:T(8,128)S(1)} %copy-done.3, f32[128,128]{1,0:T(8,128)S(1)} %broadcast_subtract_fusion, f32[16,128,128]{2,1,0:T(8,128)} %bitcast.131, ...), kind=kOutput, calls=%fused_computation.18 | convolution fusion | flops 404748288 | bytes 3354624 | tf_op jit(solution)/shard_map/dot_general | solution.py:26
  176.7 1.8 all_gather.7
  178.5 0.9 fusion.50
  179.5 2.2 fusion.19
  181.7 1.6 copy.69
  183.3 69.4 %reduce-scatter.11.cloned.1.call-done = f32[16,128]{1,0:T(8,128)} async-done(((f32[16,2048]{1,0:T(8,128)}), f32[16,128]{1,0:T(8,128)}) %reduce-scatter.11.cloned.1.call-update) | async-done | bytes 8208 | tf_op jit(solution)/shard_map/reduce_scatter | solution.py:49
  252.7 0.7 fusion.45
  253.5 1.6 copy.70
  (46 shorter events, 1.1 us)
Async XLA Ops:
  7.2 36.5 %copy-start = (bf16[256,2048]{1,0:T(8,128)(2,1)S(1)}, bf16[256,2048]{1,0:T(8,128)(2,1)}, u32[]{:S(2)}) copy-start(bf16[256,2048]{1,0:T(8,128)(2,1)} %param.17) | copy-start | bytes 3145732
  8.6 35.0 %all-to-all-start = ((bf16[16,16,128]{2,1,0:T(8,128)(2,1)}), bf16[16,16,128]{2,1,0:T(8,128)(2,1)S(1)}, u32[]{:S(2)}, u32[]{:S(2)}) async-start(bf16[16,16,128]{2,1,0:T(8,128)(2,1)} %stack.7), calls=%async_computation | async-start | bytes 131072 | tf_op jit(solution)/shard_map/all_to_all | solution.py:32
  17.0 0.7 copy-start.8
  17.0 36.6 %reduce-scatter.5.cloned.1.call-start = ((), (), s32[]{:S(2)}) async-start(), calls=%async_computation.6 | async-start | bytes 24576 | tf_op jit(solution)/shard_map/reduce_scatter | solution.py:40
  17.6 0.7 copy-start.9
  17.6 0.7 copy-start.12
  18.3 0.7 copy-start.10
  19.0 0.7 copy-start.11
  19.6 23.9 %copy-start.7 = (s32[2,16]{1,0:T(2,128)S(1)}, s32[2,16]{1,0:T(2,128)}, u32[]{:S(2)}) copy-start(s32[2,16]{1,0:T(2,128)} %param.25) | copy-start | bytes 388
  19.9 33.7 %copy-start.1 = (f32[128,16,128]{2,1,0:T(8,128)S(1)}, f32[128,16,128]{2,1,0:T(8,128)}, u32[]{:S(2)}) copy-start(f32[128,16,128]{2,1,0:T(8,128)} %param.15) | copy-start | bytes 3145732
  44.6 0.7 copy-start.5
  45.3 8.3 %copy-start.6 = (f32[128]{0:T(128)S(1)}, f32[128]{0:T(128)}, u32[]{:S(2)}) copy-start(f32[128]{0:T(128)} %param.19) | copy-start | bytes 1540
  59.0 14.3 %all-to-all-start.1 = ((bf16[16,16,128]{2,1,0:T(8,128)(2,1)}), bf16[16,16,128]{2,1,0:T(8,128)(2,1)S(1)}, u32[]{:S(2)}, u32[]{:S(2)}) async-start(bf16[16,16,128]{2,1,0:T(8,128)(2,1)} %stack.8), calls=%async_computation.2 | async-start | bytes 131072 | tf_op jit(solution)/shard_map/all_to_all | solution.py:32
  65.7 14.0 %reduce-scatter.7.cloned.1.call-start = ((), (), s32[]{:S(2)}) async-start(), calls=%async_computation.7 | async-start | bytes 24576 | tf_op jit(solution)/shard_map/reduce_scatter | solution.py:40
  74.3 95.2 %reduce-scatter.9.cloned.1.call-start = ((), (), s32[]{:S(2)}) async-start(), calls=%async_computation.8 | async-start | bytes 139264 | tf_op jit(solution)/shard_map/reduce_scatter | solution.py:49
  80.1 0.7 copy-start.4
  83.8 2.6 %copy-start.2 = (f32[2048,128]{1,0:T(8,128)S(1)}, f32[2048,128]{1,0:T(8,128)}, u32[]{:S(2)}) copy-start(f32[2048,128]{1,0:T(8,128)} %copy.60) | copy-start | bytes 3145732
  92.5 160.3 %reduce-scatter.11.cloned.1.call-start = ((), (), s32[]{:S(2)}) async-start(), calls=%async_computation.9 | async-start | bytes 139264 | tf_op jit(solution)/shard_map/reduce_scatter | solution.py:49
  171.5 2.5 copy-start.3
Sparse Core Ops, SparseCore 0:
  44.8 8.7 reduce-scatter.4
  74.4 4.2 reduce-scatter.6
  92.6 76.8 reduce-scatter.8
  179.6 73.1 reduce-scatter.10
